TPU v7x, 32 devices: a whole 2x2x4 slice. The times are simulated.
32 devices in a mesh: batch: 2 (over core), expert: 4 (over y, x), dim: 4 (over z).
Axes of the slice: x: 2, y: 2, z: 4, core: 2. Of those that a mesh axis runs over, the one named last changes fastest.
Arguments:
- inputs: bfloat16 [2048, 4096], P('batch', 'dim'), may hold values from -6 to 6
- expert_ids: int32 [2048, 4], P('batch'), may hold values from 0 to 7, all different within a row; in each aligned block of 1024 rows (0 to 1023, 1024 to 2047, ...) at most 1024 rows name the same one
- gate_weight: bfloat16 [4096, 8], P('dim'), may hold values from -0.09375 to 0.09375
- reduce_weight: bfloat16 [8, 4096, 256], P('expert', ('dim', 'batch')), may hold values from -0.09375 to 0.09375
- middle_weight: bfloat16 [8, 256, 256], P('expert', 'batch'), may hold values from -0.375 to 0.375
- expand_weight: bfloat16 [8, 4096, 256], P('expert', ('dim', 'batch')), may hold values from -0.375 to 0.375
- bias: float32 [4096], P('dim'), may hold values from -3 to 3
Outputs:
- crossed: bfloat16 [2048, 4096], P(('batch', 'expert'), 'dim')
Inputs may be any that keep to these rules, and one draw needn't show every extreme that they name: `expert_ids`: each row names 4 different experts; in each aligned block of 1024 rows (the examples of one index of batch) no expert is named by more than 1024 rows, and in some block one expert is named by exactly 1024 rows.
All inputs are finite; a program needn't handle non-finite values.
Results may differ from a plain program's by a relative error of at most 0.012.
Values may be sent and summed in bfloat16 or wider, within the bound.
No kernel may reach another device: no remote copies, remote signals or barrier semaphores. Data moves between devices by JAX's collectives and lax.ppermute only.
A program may use at most 64 MiB of HBM per device.

v0:
```python
import jax
import jax.numpy as jnp
from jax import lax
from jax.sharding import PartitionSpec as P

CAP = 1024


def pick_rows(expert_rows, slot_pick):
    return expert_rows[slot_pick]


def on_device(inputs, expert_ids, gate_weight, reduce_weight, middle_weight, expand_weight, bias):
    tok_count, feature_width = inputs.shape
    local_count = reduce_weight.shape[0]
    all_experts = gate_weight.shape[1]
    first_expert = lax.axis_index("expert") * local_count
    numbers = jnp.arange(all_experts, dtype=jnp.int32)
    chosen = jnp.sum((expert_ids[:, :, None] == numbers[None, None, :]).astype(jnp.int32), axis=1)
    position = jnp.cumsum(chosen, axis=0) - chosen
    chosen_here = lax.dynamic_slice_in_dim(chosen, first_expert, local_count, 1)
    position_here = lax.dynamic_slice_in_dim(position, first_expert, local_count, 1)
    target = jnp.where(chosen_here > 0, position_here, CAP).T
    expert_grid = jnp.broadcast_to(
        jnp.arange(local_count, dtype=jnp.int32)[:, None], (local_count, tok_count)
    )
    token_grid = jnp.broadcast_to(
        jnp.arange(tok_count, dtype=jnp.int32)[None, :], (local_count, tok_count)
    )
    slot_owner = (
        jnp.full((local_count, CAP), tok_count, jnp.int32)
        .at[expert_grid, target]
        .set(token_grid, mode="drop")
    )
    padded = jnp.concatenate([inputs, jnp.zeros((1, feature_width), inputs.dtype)], axis=0)
    dispatched = padded[slot_owner]
    logits_part = jnp.dot(inputs, gate_weight, preferred_element_type=jnp.float32)
    projected = jnp.einsum(
        "esd,edr->esr",
        dispatched,
        lax.all_gather(reduce_weight, "batch", axis=1, tiled=True),
        preferred_element_type=jnp.float32,
    )
    middle_full = lax.all_gather(middle_weight, "batch", axis=1, tiled=True)
    logits, summed = (
        lax.psum(logits_part.astype(jnp.bfloat16), "dim").astype(jnp.float32),
        lax.psum(projected.astype(jnp.bfloat16), "dim").astype(jnp.float32),
    )
    squashed = jnp.tanh(summed).astype(jnp.bfloat16)
    inner_mix = jnp.einsum(
        "esj,eij->esi", squashed, middle_full, preferred_element_type=jnp.float32
    )
    hidden = jnp.tanh(inner_mix).astype(jnp.bfloat16)
    expanded = jnp.einsum(
        "esr,edr->esd",
        hidden,
        lax.all_gather(expand_weight, "batch", axis=1, tiled=True),
        preferred_element_type=jnp.float32,
    )
    gate_values = jax.nn.sigmoid(
        lax.dynamic_slice_in_dim(logits, first_expert, local_count, 1)
    ) * chosen_here.astype(jnp.float32)
    slot_read = jnp.minimum(position_here, CAP - 1).T
    picked = jax.vmap(pick_rows)(expanded, slot_read)
    expert_mix = jnp.sum(gate_values.T[:, :, None] * (picked + bias[None, None, :]), axis=0)
    partial_term = inputs.astype(jnp.float32) * expert_mix
    summed_rows = lax.psum_scatter(
        partial_term.astype(jnp.bfloat16), "expert", scatter_dimension=0, tiled=True
    ).astype(jnp.float32)
    row_count = summed_rows.shape[0]
    own_rows = lax.dynamic_slice_in_dim(inputs, lax.axis_index("expert") * row_count, row_count, 0)
    return (own_rows.astype(jnp.float32) + summed_rows).astype(jnp.bfloat16)


def solution(mesh):
    in_specs = (
        P("batch", "dim"),
        P("batch", None),
        P("dim", None),
        P("expert", ("dim", "batch"), None),
        P("expert", "batch", None),
        P("expert", ("dim", "batch"), None),
        P("dim"),
    )
    out_specs = P(("batch", "expert"), "dim")
    return jax.shard_map(
        on_device, mesh=mesh, in_specs=in_specs, out_specs=out_specs, check_vma=False
    )
```

profile of v0, /device:TPU:0, one launch (start us, length us, event | category | flops | bytes accessed | tf_op | source)
XLA Modules:
  0.0 194.0 jit_solution(1393359733203876569)
XLA Ops:
  6.5 0.7 all-gather.3.cloned.1.call-update
  7.3 0.0 all-gather.5.cloned.1.call-start
  7.3 0.7 all-gather.5.cloned.1.call-update
  8.0 0.0 all-reduce.3.cloned.1.call-start
  8.1 0.7 convert_reduce_fusion
  8.8 2.3 %reduce-window.6 = s32[8,8,128]{2,1,0:T(8,128)S(1)} reduce-window(s32[8,8,128]{2,1,0:T(8,128)S(1)} %copy.12, s32[]{:T(128)} %constant.15.clone.1), window={size=1x1x128 pad=0_0x0_0x127_0}, to_apply=%region_2.3 | reduce-window | flops 1040384 | bytes 65540 | tf_op jit(solution)/shard_map/reduce-window
  11.1 0.3 slice_reduce_fusion
  11.4 0.2 reduce-window.9
  11.6 0.1 add_bitcast_fusion
  11.7 0.8 and_reduce_fusion
  12.4 0.7 multiply_reduce_fusion.1
  13.2 8.0 %scatter_custom_fusion = s32[2048]{0:T(1024)S(1)} fusion(s32[2048]{0:T(1024)S(1)} %get-tuple-element.6, s32[2048]{0:T(1024)S(1)} %get-tuple-element.5, s32[]{:T(128)} %constant.5.clone.1), kind=kCustom, calls=%fused_computation.40 | custom fusion | bytes 8196
  21.3 1.8 concatenate.6
  23.1 9.7 %gather_fusion = bf16[2048,1024]{1,0:T(8,128)(2,1)} fusion(bf16[1025,1024]{1,0:T(8,128)(2,1)S(1)} %concatenate.6, s32[2048]{0:T(1024)S(1)} %bitcast_clamp_fusion), kind=kCustom, calls=%fused_computation | custom fusion | bytes 8396800 | tf_op jit(solution)/shard_map/gather | solution.py:36
  32.8 4.9 %convolution_convert_fusion = bf16[2,1024,256]{2,1,0:T(8,128)(2,1)} fusion(bf16[2,1024,1024]{2,1,0:T(8,128)(2,1)} %bitcast.61, bf16[2,1024,256]{2,1,0:T(8,128)(2,1)} %all-gather.3.cloned.1.call-done), kind=kOutput, calls=%fused_computation.7 | convolution fusion | flops 1074266112 | bytes 6291456 | tf_op jit(solution)/shard_map/esd,edr->esr/dot_general | solution.py:38
  37.7 0.0 all-reduce.3.cloned.1.call-update
  37.7 0.0 reduce-scatter.2.cloned.1.call-start
  37.8 0.0 copy-done
  37.8 0.0 copy-done.1
  37.8 0.6 convolution_convert_fusion.1
  38.4 21.4 %psum.14 = bf16[1024,8]{0,1:T(8,128)(2,1)S(1)} all-reduce(bf16[1024,8]{0,1:T(8,128)(2,1)S(1)} %convolution_convert_fusion.1), channel_id=1, replica_groups=mesh['batch'=2,'expert'=4,'dim'=4] {'dim'}, use_global_device_ids=true, to_apply=%region_0.0 | all-reduce | flops 8192 | bytes 32768 | tf_op jit(solution)/shard_map/psum | solution.py:46
  59.9 0.0 copy-done.2
  59.9 2.0 %all_gather.10 = bf16[2,256,256]{2,1,0:T(8,128)(2,1)S(1)} all-gather(bf16[2,128,256]{2,1,0:T(8,128)(2,1)S(1)} %copy-done.2), channel_id=1, replica_groups=mesh['batch'=2,'expert'=4,'dim'=4] {'batch'}, dimensions={1}, use_global_device_ids=true | all-gather | bytes 393216 | tf_op jit(solution)/shard_map/all_gather | solution.py:44
  61.9 0.0 all-gather.5.cloned.1.call-done
  61.9 30.9 %all-reduce.3.cloned.1.call-done = bf16[2,1024,256]{2,1,0:T(8,128)(2,1)} async-done(((bf16[2,1024,256]{2,1,0:T(8,128)(2,1)}), bf16[2,1024,256]{2,1,0:T(8,128)(2,1)}) %all-reduce.3.cloned.1.call-update) | async-done | bytes 1048592 | tf_op jit(solution)/shard_map/psum | solution.py:47
  92.8 6.5 %fusion = f32[2,1024,1024]{2,1,0:T(8,128)} fusion(bf16[2,1024,256]{2,1,0:T(8,128)(2,1)} %all-gather.5.cloned.1.call-done, bf16[2,256,256]{2,1,0:T(8,128)(2,1)S(1)} %all_gather.10, bf16[2,1024,256]{2,1,0:T(8,128)(2,1)} %all-reduce.3.cloned.1.call-done), kind=kOutput, calls=%fused_computation.8 | convolution fusion | flops 1343750144 | bytes 10747904 | tf_op jit(solution)/shard_map/esr,edr->esd/dot_general | solution.py:54
  99.3 44.0 %gather_fusion.1 = f32[2048,1024]{1,0:T(8,128)} fusion(f32[2,1024,1024]{2,1,0:T(8,128)} %fusion, s32[2048]{0:T(1024)S(1)} %bitcast.59), kind=kCustom, calls=%fused_computation.1 | custom fusion | bytes 16793600 | tf_op jit(solution)/shard_map/vmap()/gather | solution.py:10
  143.3 4.3 %multiply_reduce_fusion = f32[1024,1024]{1,0:T(8,128)S(1)} fusion(f32[2,1024,1024]{2,1,0:T(8,128)} %bitcast.60, f32[1024]{0:T(1024)S(1)} %copy-done.3, f32[2,1024]{1,0:T(2,128)S(1)} %fusion.9), kind=kLoop, calls=%fused_computation.3 | loop fusion | flops 5242880 | bytes 12595200 | tf_op jit(solution)/shard_map/reduce_sum | solution.py:65
  147.5 2.2 %multiply_convert_fusion = bf16[1024,1024]{1,0:T(8,128)(2,1)} fusion(f32[1024,1024]{1,0:T(8,128)S(1)} %multiply_reduce_fusion, bf16[1024,1024]{1,0:T(8,128)(2,1)S(1)} %copy-done.1), kind=kLoop, calls=%fused_computation.4 | loop fusion | flops 3145728 | bytes 8388608 | tf_op jit(solution)/shard_map/convert_element_type | solution.py:68
  149.8 0.0 reduce-scatter.2.cloned.1.call-update
  149.8 35.6 %reduce-scatter.2.cloned.1.call-done = bf16[256,1024]{1,0:T(8,128)(2,1)} async-done(((bf16[1024,1024]{1,0:T(8,128)(2,1)}), bf16[256,1024]{1,0:T(8,128)(2,1)}) %reduce-scatter.2.cloned.1.call-update) | async-done | bytes 524304 | tf_op jit(solution)/shard_map/reduce_scatter | solution.py:67
  185.4 2.0 %add_convert_fusion = bf16[256,1024]{1,0:T(8,128)(2,1)} fusion(bf16[256,1024]{1,0:T(8,128)(2,1)} %reduce-scatter.2.cloned.1.call-done, bf16[1024,1024]{1,0:T(8,128)(2,1)S(1)} %copy-done.1, s32[]{:T(128)S(6)} %select_n.23), kind=kLoop, calls=%fused_computation.10 | loop fusion | flops 1048576 | bytes 1572868 | tf_op jit(solution)/shard_map/convert_element_type | solution.py:72
  (20 shorter events, 0.2 us)
Async XLA Ops:
  6.5 31.2 %copy-start = (bf16[1024,8]{0,1:T(8,128)(2,1)S(1)}, bf16[1024,8]{0,1:T(8,128)(2,1)}, u32[]{:S(2)}) copy-start(bf16[1024,8]{0,1:T(8,128)(2,1)} %param.9) | copy-start | bytes 49156
  6.5 26.2 %all-gather.3.cloned.1.call-start = ((), (), s32[]{:S(2)}) async-start(), calls=%async_computation.1 | async-start | bytes 1572864 | tf_op jit(solution)/shard_map/all_gather | solution.py:41
  7.3 54.7 %all-gather.5.cloned.1.call-start = ((), (), s32[]{:S(2)}) async-start(), calls=%async_computation.3 | async-start | bytes 1572864 | tf_op jit(solution)/shard_map/all_gather | solution.py:57
  8.0 84.8 %all-reduce.3.cloned.1.call-start = ((), (), s32[]{:S(2)}) async-start(), calls=%async_computation.2 | async-start | bytes 2097152 | tf_op jit(solution)/shard_map/psum | solution.py:47
  32.8 5.0 %copy-start.1 = (bf16[1024,1024]{1,0:T(8,128)(2,1)S(1)}, bf16[1024,1024]{1,0:T(8,128)(2,1)}, u32[]{:S(2)}) copy-start(bf16[1024,1024]{1,0:T(8,128)(2,1)} %param.7) | copy-start | bytes 6291460
  32.8 27.1 %copy-start.2 = (bf16[2,128,256]{2,1,0:T(8,128)(2,1)S(1)}, bf16[2,128,256]{2,1,0:T(8,128)(2,1)}, u32[]{:S(2)}) copy-start(bf16[2,128,256]{2,1,0:T(8,128)(2,1)} %param.11) | copy-start | bytes 393220
  37.7 147.7 %reduce-scatter.2.cloned.1.call-start = ((), (), s32[]{:S(2)}) async-start(), calls=%async_computation.4 | async-start | bytes 2621440 | tf_op jit(solution)/shard_map/reduce_scatter | solution.py:67
  99.3 44.0 %copy-start.3 = (f32[1024]{0:T(1024)S(1)}, f32[1024]{0:T(1024)}, u32[]{:S(2)}) copy-start(f32[1024]{0:T(1024)} %param.13) | copy-start | bytes 12292
Sparse Core Ops, SparseCore 0:
  8.9 11.7 all-gather.2
  22.2 10.1 all-gather.4
  37.8 54.9 all-reduce.2
  149.9 35.4 reduce-scatter.1
where the time goes:
time: 195 us; the launch traced here: 194 us
  waiting for transfers between devices  68 us (35%)
  local copies, waits for them, and re-layouts  63.8 us (33%)
  blocking collectives  23.4 us (12%)
  other arithmetic  13.4 us (7%)
  between operations  13.3 us (7%)
  matrix products  12 us (6%)
    gather x1, local copies, waits for them, and re-layouts, pick_rows(): return expert_rows[slot_pick]  44 us
    reduce_scatter x1, waiting for transfers between devices, on_device(): lax.psum_scatter(partial_term.astype(jnp.bfloat16), 'expert', scatter_dim...  35.6 us
    psum x1, waiting for transfers between devices, on_device(): lax.psum(projected.astype(jnp.bfloat16), 'dim').astype(jnp.float32)  30.9 us
    psum x1, blocking collectives, on_device(): lax.psum(logits_part.astype(jnp.bfloat16), 'dim').astype(jnp.float32)  21.4 us
    gather x1, local copies, waits for them, and re-layouts, on_device(): dispatched = padded[slot_owner]  9.67 us
    unnamed x12, local copies, waits for them, and re-layouts  8.09 us
    dot_general x1, matrix products, on_device(): jnp.einsum('esr,edr->esd', hidden, lax.all_gather(expand_weight, 'batch',...  6.48 us
    dot_general x1, matrix products, on_device(): jnp.einsum('esd,edr->esr', dispatched, lax.all_gather(reduce_weight, 'bat...  4.9 us
  transfers between devices with their start and end apart: 4, of which 2 were waited for; matrix products, arithmetic and copies ran while one was open for 16% of the time, Pallas kernels for 0%

commit v1 on v0

--- a/solution.py
+++ b/solution.py
@@ -44,7 +44,9 @@
     middle_full = lax.all_gather(middle_weight, "batch", axis=1, tiled=True)
     logits, summed = (
         lax.psum(logits_part.astype(jnp.bfloat16), "dim").astype(jnp.float32),
-        lax.psum(projected.astype(jnp.bfloat16), "dim").astype(jnp.float32),
+        jnp.sum(jax.lax.all_gather(projected.astype(jnp.bfloat16), axis_name="dim"), 0).astype(
+            jnp.float32
+        ),
     )
     squashed = jnp.tanh(summed).astype(jnp.bfloat16)
     inner_mix = jnp.einsum(

time: 195 us -> 234 us (1.20)
  waiting for transfers between devices: 68 us -> 104 us
  other arithmetic: 13.4 us -> 16.5 us
    all_gather x0 -> x1, waiting for transfers between devices: none -> 59 us  [on_device(): jax.lax.all_gather(projected.astype(jnp.bfloat16), axis_name='dim')]
    psum x1 -> x0, waiting for transfers between devices: 30.9 us -> none  [on_device(): lax.psum(projected.astype(jnp.bfloat16), 'dim').astype(jnp.float32)]
    all_gather x1, waiting for transfers between devices: 0.02 us -> 5.93 us  [on_device(): lax.all_gather(expand_weight, 'batch', axis=1, tiled=True)]
    reduce_sum x0 -> x1, other arithmetic: none -> 3.17 us  [on_device(): jnp.sum(jax.lax.all_gather(projected.astype(jnp.bfloat16), axis_name='dim...]
  transfers between devices with their start and end apart: 4 -> 4, of which waited for: 2 -> 3; matrix products, arithmetic and copies ran while one was open for 16% -> 12% of each run, Pallas kernels for 0% -> 0%
where the time goes in v1:
time: 234 us; the launch traced here: 233 us
  waiting for transfers between devices  104 us (44%)
  local copies, waits for them, and re-layouts  63.8 us (27%)
  blocking collectives  23.3 us (10%)
  other arithmetic  16.5 us (7%)
  between operations  13.3 us (6%)
  matrix products  11.7 us (5%)
    all_gather x1, waiting for transfers between devices, on_device(): jax.lax.all_gather(projected.astype(jnp.bfloat16), axis_name='dim')  59 us
    gather x1, local copies, waits for them, and re-layouts, pick_rows(): return expert_rows[slot_pick]  44 us
    reduce_scatter x1, waiting for transfers between devices, on_device(): lax.psum_scatter(partial_term.astype(jnp.bfloat16), 'expert', scatter_dim...  37.5 us
    psum x1, blocking collectives, on_device(): lax.psum(logits_part.astype(jnp.bfloat16), 'dim').astype(jnp.float32)  21.3 us
    gather x1, local copies, waits for them, and re-layouts, on_device(): dispatched = padded[slot_owner]  9.67 us
    unnamed x12, local copies, waits for them, and re-layouts  8.09 us
    dot_general x1, matrix products, on_device(): jnp.einsum('esr,edr->esd', hidden, lax.all_gather(expand_weight, 'batch',...  6.18 us
    all_gather x1, waiting for transfers between devices, on_device(): lax.all_gather(expand_weight, 'batch', axis=1, tiled=True)  5.93 us
  transfers between devices with their start and end apart: 4, of which 3 were waited for; matrix products, arithmetic and copies ran while one was open for 12% of the time, Pallas kernels for 0%

profile of v1, /device:TPU:0, one launch (start us, length us, event | category | flops | bytes accessed | tf_op | source)
XLA Modules:
  0.0 232.5 jit_solution(11750584277455326027)
XLA Ops:
  6.5 0.7 all-gather.5.cloned.1.call-update
  7.3 0.0 all-gather.9.cloned.1.call-start
  7.3 0.7 convert_reduce_fusion
  8.1 2.3 reduce-window.6
  10.3 0.3 slice_reduce_fusion
  10.6 0.2 reduce-window.9
  10.8 0.1 add_bitcast_fusion
  10.9 0.7 multiply_reduce_fusion.1
  11.7 0.8 and_reduce_fusion
  12.5 8.0 %scatter_custom_fusion = s32[2048]{0:T(1024)S(1)} fusion(s32[2048]{0:T(1024)S(1)} %get-tuple-element.6, s32[2048]{0:T(1024)S(1)} %get-tuple-element.5, s32[]{:T(128)} %constant.6.clone.1), kind=kCustom, calls=%fused_computation.40 | custom fusion | bytes 8196
  20.5 1.8 concatenate.6
  22.3 9.7 %gather_fusion = bf16[2048,1024]{1,0:T(8,128)(2,1)} fusion(bf16[1025,1024]{1,0:T(8,128)(2,1)S(1)} %concatenate.6, s32[2048]{0:T(1024)S(1)} %bitcast_clamp_fusion), kind=kCustom, calls=%fused_computation | custom fusion | bytes 8396800 | tf_op jit(solution)/shard_map/gather | solution.py:36
  32.0 4.9 %convolution_convert_fusion = bf16[2,1024,256]{2,1,0:T(8,128)(2,1)} fusion(bf16[2,1024,1024]{2,1,0:T(8,128)(2,1)} %bitcast.62, bf16[2,1024,256]{2,1,0:T(8,128)(2,1)} %all-gather.5.cloned.1.call-done), kind=kOutput, calls=%fused_computation.7 | convolution fusion | flops 1074266112 | bytes 6291456 | tf_op jit(solution)/shard_map/esd,edr->esr/dot_general | solution.py:38
  36.9 0.0 all-gather.9.cloned.1.call-update
  36.9 0.0 all-gather.7.cloned.1.call-start
  36.9 0.7 all-gather.7.cloned.1.call-update
  37.6 0.0 reduce-scatter.2.cloned.1.call-start
  37.7 0.0 copy-done
  37.7 0.0 copy-done.1
  37.7 0.6 convolution_convert_fusion.1
  38.4 21.3 %psum.7 = bf16[1024,8]{0,1:T(8,128)(2,1)S(1)} all-reduce(bf16[1024,8]{0,1:T(8,128)(2,1)S(1)} %convolution_convert_fusion.1), channel_id=1, replica_groups=mesh['batch'=2,'expert'=4,'dim'=4] {'dim'}, use_global_device_ids=true, to_apply=%region_0.0 | all-reduce | flops 8192 | bytes 32768 | tf_op jit(solution)/shard_map/psum | solution.py:46
  59.7 2.0 all_gather.18
  61.7 59.0 %all-gather.9.cloned.1.call-done = bf16[8,1024,256]{2,1,0:T(8,128)(2,1)} async-done(((bf16[2,1024,256]{2,1,0:T(8,128)(2,1)}), bf16[8,1024,256]{2,1,0:T(8,128)(2,1)}) %all-gather.9.cloned.1.call-update) | async-done | bytes 4194320 | tf_op jit(solution)/shard_map/all_gather | solution.py:47
  120.7 3.2 %reduce_sum.31 = bf16[2,1024,256]{2,1,0:T(8,128)(2,1)S(1)} reduce(bf16[4,2,1024,256]{3,2,1,0:T(8,128)(2,1)} %bitcast.63, bf16[]{:T(256)} %constant.10.clone.1), dimensions={0}, to_apply=%region_5.6 | reduce | flops 1572864 | bytes 5242882 | tf_op jit(solution)/shard_map/reduce_sum | solution.py:47
  123.9 5.9 %all-gather.7.cloned.1.call-done = bf16[2,1024,256]{2,1,0:T(8,128)(2,1)} async-done(((bf16[2,512,256]{2,1,0:T(8,128)(2,1)}), bf16[2,1024,256]{2,1,0:T(8,128)(2,1)}) %all-gather.7.cloned.1.call-update) | async-done | bytes 1048592 | tf_op jit(solution)/shard_map/all_gather | solution.py:59
  129.8 6.2 %fusion = f32[2,1024,1024]{2,1,0:T(8,128)} fusion(bf16[2,1024,256]{2,1,0:T(8,128)(2,1)} %all-gather.7.cloned.1.call-done, bf16[2,256,256]{2,1,0:T(8,128)(2,1)S(1)} %all_gather.18, bf16[2,1024,256]{2,1,0:T(8,128)(2,1)S(1)} %reduce_sum.31), kind=kOutput, calls=%fused_computation.8 | convolution fusion | flops 1343750144 | bytes 10747904 | tf_op jit(solution)/shard_map/esr,edr->esd/dot_general | solution.py:56
  136.0 44.0 %gather_fusion.1 = f32[2048,1024]{1,0:T(8,128)} fusion(f32[2,1024,1024]{2,1,0:T(8,128)} %fusion, s32[2048]{0:T(1024)S(1)} %bitcast.60), kind=kCustom, calls=%fused_computation.1 | custom fusion | bytes 16793600 | tf_op jit(solution)/shard_map/vmap()/gather | solution.py:10
  180.0 4.3 %multiply_reduce_fusion = f32[1024,1024]{1,0:T(8,128)S(1)} fusion(f32[2,1024,1024]{2,1,0:T(8,128)} %bitcast.61, f32[1024]{0:T(1024)S(1)} %copy-done.3, f32[2,1024]{1,0:T(2,128)S(1)} %fusion.9), kind=kLoop, calls=%fused_computation.3 | loop fusion | flops 5242880 | bytes 12595200 | tf_op jit(solution)/shard_map/reduce_sum | solution.py:67
  184.3 2.2 multiply_convert_fusion
  186.5 0.0 reduce-scatter.2.cloned.1.call-update
  186.5 37.5 %reduce-scatter.2.cloned.1.call-done = bf16[256,1024]{1,0:T(8,128)(2,1)} async-done(((bf16[1024,1024]{1,0:T(8,128)(2,1)}), bf16[256,1024]{1,0:T(8,128)(2,1)}) %reduce-scatter.2.cloned.1.call-update) | async-done | bytes 524304 | tf_op jit(solution)/shard_map/reduce_scatter | solution.py:69
  224.0 2.0 add_convert_fusion
  (21 shorter events, 0.2 us)
Async XLA Ops:
  6.5 31.2 %copy-start = (bf16[1024,8]{0,1:T(8,128)(2,1)S(1)}, bf16[1024,8]{0,1:T(8,128)(2,1)}, u32[]{:S(2)}) copy-start(bf16[1024,8]{0,1:T(8,128)(2,1)} %param.9) | copy-start | bytes 49156
  6.5 25.5 %all-gather.5.cloned.1.call-start = ((), (), s32[]{:S(2)}) async-start(), calls=%async_computation.1 | async-start | bytes 1572864 | tf_op jit(solution)/shard_map/all_gather | solution.py:41
  7.3 113.5 %all-gather.9.cloned.1.call-start = ((), (), s32[]{:S(2)}) async-start(), calls=%async_computation.4 | async-start | bytes 5242880 | tf_op jit(solution)/shard_map/all_gather | solution.py:47
  32.0 5.7 %copy-start.1 = (bf16[1024,1024]{1,0:T(8,128)(2,1)S(1)}, bf16[1024,1024]{1,0:T(8,128)(2,1)}, u32[]{:S(2)}) copy-start(bf16[1024,1024]{1,0:T(8,128)(2,1)} %param.7) | copy-start | bytes 6291460
  32.0 27.7 %copy-start.2 = (bf16[2,128,256]{2,1,0:T(8,128)(2,1)S(1)}, bf16[2,128,256]{2,1,0:T(8,128)(2,1)}, u32[]{:S(2)}) copy-start(bf16[2,128,256]{2,1,0:T(8,128)(2,1)} %param.11) | copy-start | bytes 393220
  36.9 92.9 %all-gather.7.cloned.1.call-start = ((), (), s32[]{:S(2)}) async-start(), calls=%async_computation.2 | async-start | bytes 1572864 | tf_op jit(solution)/shard_map/all_gather | solution.py:59
  37.6 186.4 %reduce-scatter.2.cloned.1.call-start = ((), (), s32[]{:S(2)}) async-start(), calls=%async_computation.3 | async-start | bytes 2621440 | tf_op jit(solution)/shard_map/reduce_scatter | solution.py:69
  136.0 44.0 %copy-start.3 = (f32[1024]{0:T(1024)S(1)}, f32[1024]{0:T(1024)}, u32[]{:S(2)}) copy-start(f32[1024]{0:T(1024)} %param.13) | copy-start | bytes 12292
Sparse Core Ops, SparseCore 0:
  8.9 11.7 all-gather.4
  37.0 83.6 all-gather.8
  122.3 7.5 all-gather.6
  186.6 37.3 reduce-scatter.1
